TPU v7x, 32 devices: a whole 2x2x4 slice. The times are simulated.
32 devices in a mesh: blk: 8 (over z, y), rep: 4 (over x, core).
Axes of the slice: x: 2, y: 2, z: 4, core: 2. Of those that a mesh axis runs over, the one named last changes fastest.
Arguments:
- embeddings: bfloat16 [3072, 1024], P(('blk', 'rep')), may hold values from -60 to 60, as said below
Outputs:
- nearest: float32 [3072, 8], P(('blk', 'rep'))
- dup_count: float32 [3072], P(('blk', 'rep'))
Inputs may be any that keep to these rules, and one draw needn't show every extreme that they name: Real-valued embeddings; no row is zero.
All inputs are finite; a program needn't handle non-finite values.
Results may differ from a plain program's by a relative error of at most 0.00068.
Values may be sent and summed in bfloat16 or wider, within the bound.
A program may use at most 128 MiB of HBM per device.

v0:
```python
import math

import jax
import jax.numpy as jnp
from jax import lax
from jax.experimental import pallas as pl
from jax.experimental.pallas import tpu as pltpu
from jax.sharding import PartitionSpec as P

TOPK = 8
SUB, LANES = 8, 128


decision_bound = 0.5
sigmoid_sharpness = 0.05


def joined(shard, axis, combine):
    everything = jax.tree.map(lambda part: lax.all_gather(part, axis), shard)
    initial = jax.tree.map(lambda part: part[0], everything)

    def lap(k, so_far):
        return combine(so_far, jax.tree.map(lambda part: part[k], everything))

    return lax.fori_loop(1, lax.axis_size(axis), lap, initial)


def unit_rows(block):
    whole = block.astype(jnp.float32)
    return (whole / jnp.sqrt(jnp.sum(whole * whole, axis=1, keepdims=True) + 1e-06)).astype(
        jnp.bfloat16
    )


def top_values(table):
    columns = lax.broadcasted_iota(jnp.int32, table.shape, 1)
    picked = []
    for rank in range(TOPK):
        largest = jnp.max(table, axis=1)
        first_hit = jnp.min(jnp.where(table == largest[:, None], columns, table.shape[1]), axis=1)
        table = jnp.where(columns == first_hit[:, None], -jnp.inf, table)
        picked.append(largest)
    return jnp.stack(picked, axis=1)


def score(queries, query_ids, keys, key_ids, carry):
    cosine_table = lax.dot_general(
        queries, keys, (((1,), (1,)), ((), ())), preferred_element_type=jnp.float32
    )
    cosine_table = jnp.where(query_ids[:, None] == key_ids[None, :], -2.0, cosine_table)
    best = top_values(jnp.concatenate([carry[0], cosine_table], axis=1))
    duplicate_tally = jnp.sum(
        jax.nn.sigmoid((cosine_table - decision_bound) / sigmoid_sharpness), axis=1
    )
    return (best, duplicate_tally)


def join_lists(first, runner_value):
    best = top_values(jnp.concatenate([first[0], runner_value[0]], axis=1))
    return (best, first[1] + runner_value[1])


def body(embeddings):
    rows = embeddings.shape[0]
    reps = lax.axis_size("rep")
    copy_number = lax.axis_index("rep")
    tile_number = lax.axis_index("blk")
    unit = unit_rows(embeddings)
    queries = lax.all_gather(unit, "rep", axis=0, tiled=True)
    query_ids = tile_number * reps * rows + jnp.arange(reps * rows, dtype=jnp.int32)
    start_lists = (
        jnp.full((reps * rows, TOPK), -2.0, jnp.float32),
        jnp.zeros((reps * rows,), jnp.float32),
    )
    piece = lax.all_gather(unit, "blk", axis=0, tiled=True)
    position = jnp.arange(piece.shape[0], dtype=jnp.int32)
    key_ids = (position // rows * reps + copy_number) * rows + position % rows
    lists = score(queries, query_ids, piece, key_ids, start_lists)
    best, duplicate_tally = joined(lists, "rep", join_lists)
    offset = copy_number * rows
    nearest = lax.dynamic_slice_in_dim(best, offset, rows, 0)
    dup_count = lax.dynamic_slice_in_dim(duplicate_tally, offset, rows, 0)
    return (nearest, dup_count)


PLAN = {"blk": 8, "rep": 4}
PLANE = 4
CHUNKS = 3
MESH = pl.DeviceIdType.MESH

SORT8 = (
    (0, 1), (2, 3), (4, 5), (6, 7),
    (0, 2), (1, 3), (4, 6), (5, 7),
    (1, 2), (5, 6),
    (0, 4), (1, 5), (2, 6), (3, 7),
    (2, 4), (3, 5),
    (1, 2), (3, 4), (5, 6),
)


def exchange(items, pairs):
    items = list(items)
    for i, j in pairs:
        items[i], items[j] = jnp.maximum(items[i], items[j]), jnp.minimum(items[i], items[j])
    return items


def in_order(items):
    if len(items) == TOPK:
        return exchange(items, SORT8)
    pairs = [(j, j + 1) for end in range(len(items) - 1, 0, -1) for j in range(end)]
    return exchange(items, pairs)


def merged(best, other):
    size = len(other)
    best = [
        jnp.maximum(best[i], other[TOPK - 1 - i]) if TOPK - 1 - i < size else best[i]
        for i in range(TOPK)
    ]
    pairs = [
        (i, i + step) for step in (4, 2, 1) for i in range(TOPK) if i // step % 2 == 0
    ]
    return exchange(best, pairs)


def duplicates(sim):
    scale = -math.log2(math.e) / sigmoid_sharpness
    return 1.0 / (1.0 + jnp.exp2((sim - decision_bound) * scale))


def take_in(sim_ref, keys, lanes, state, fresh):
    width = min(lanes, LANES)

    def tile(t, _):
        start = 0 if lanes <= LANES else pl.multiple_of(t * LANES, LANES)
        part = pl.ds(start, width)
        best = None if fresh else [state[k, :, part] for k in range(TOPK)]
        count = jnp.zeros((SUB, width), jnp.float32) if fresh else state[TOPK, :, part]
        for group in range(0, keys, SUB * TOPK):
            rows = [
                sim_ref[pl.ds(row, SUB), part]
                for row in range(group, min(group + SUB * TOPK, keys), SUB)
            ]
            for row in rows:
                count = count + duplicates(row)
            rows = in_order(rows)
            best = rows if best is None else merged(best, rows)
        for k in range(TOPK):
            state[k, :, part] = best[k]
        state[TOPK, :, part] = count
        return 0

    if lanes <= LANES:
        tile(0, 0)
    else:
        lax.fori_loop(0, lanes // LANES, tile, 0)


def across_rows(best, count):
    for step in (4, 2, 1):
        best = merged(best, [pltpu.roll(item, step, axis=0) for item in best])
        if count is not None:
            count = count + pltpu.roll(count, step, axis=0)
    row = lax.broadcasted_iota(jnp.int32, best[0].shape, 0)
    joined_list = best[0]
    for k in range(1, TOPK):
        joined_list = jnp.where(row == k, best[k], joined_list)
    return joined_list, count


def against(keys, queries):
    return lax.dot_general(keys, queries, (((1,), (1,)), ((), ())), preferred_element_type=jnp.float32)


def direct_kernel(
    x_ref, out_ref, raw, plane, far, sim_own, sim_pair, sim_cross, sim_last,
    own_state, plane_state, cross_state, whole, result, arrived,
    raw_sem, send, recv, fwd_send, fwd_recv, res_send, res_recv,
):
    rows, width = x_ref.shape
    step = rows // CHUNKS
    blk, rep = lax.axis_index("blk"), lax.axis_index("rep")
    y, z, core, x = blk % 2, blk // 2, rep % 2, rep // 2
    inner = (z == 1) | (z == 2)

    def place(px, py, pz, other_core=0):
        return (pz * 2 + py, px * 2 + (core + other_core) % 2)

    partner = place(x, y, z, 1)
    along_x, along_y = place(1 - x, y, z), place(x, 1 - y, z)
    pair = place(x, y, z + 1 - 2 * (z % 2))
    middle = place(x, y, 3 - z)
    source = place(x, y, (1 - z // 2) * (3 - z) + z // 2 * (z - 2))
    relay_to = place(x, y, (2 - z) * 2)

    barrier = pltpu.get_barrier_semaphore()

    def greet(device):
        pl.semaphore_signal(barrier, inc=1, device_id=device, device_id_type=MESH)

    for peer in (partner, along_x, along_y, pair):
        greet(peer)

    @pl.when(inner)
    def _():
        greet(middle)

    fetch = pltpu.make_async_copy(x_ref, raw, raw_sem)
    fetch.start()
    fetch.wait()
    plane[0, 0] = unit_rows(raw[...])

    pl.semaphore_wait(barrier, 4 + z * (3 - z) // 2)

    def part(c):
        return pl.ds(c * step, step)

    def move(src, dst, send_to, recv_from, c, device):
        return pltpu.make_async_remote_copy(
            src_ref=src.at[part(c)], dst_ref=dst.at[part(c)],
            send_sem=send.at[send_to, c], recv_sem=recv.at[recv_from, c],
            device_id=device, device_id_type=MESH,
        )

    own = plane.at[0, 0]
    order = range(CHUNKS)
    backward = range(CHUNKS - 1, -1, -1)

    def to_middle(c):
        return move(own, far.at[3 - z], 3, 3 + 3 - z, c, middle)

    def relay_pair(c):
        return move(far.at[0], far.at[1], 4, 4, c, relay_to)

    def relay_transit(c):
        return move(far.at[2], far.at[1], 5, 4, c, pair)

    to_x = [move(own, plane.at[1, 0], 0, 0, c, along_x) for c in order]
    to_y = [move(own, plane.at[2, 0], 1, 1, c, along_y) for c in order]
    to_pair = [move(own, far.at[0], 2, 3, c, pair) for c in order]
    arrives = [move(far.at[0], far.at[1], 4, 4, c, pair) for c in order]
    relay_xy = [
        move(plane.at[2, 0], plane.at[3, 0], 6, 2, c, along_x)
        if c == CHUNKS - 1
        else move(plane.at[1, 0], plane.at[3, 0], 6, 2, c, along_y)
        for c in order
    ]

    @pl.when(inner)
    def _():
        for c in order:
            to_middle(c).start()

    for c, d in zip(order, backward):
        to_pair[c].start()
        to_x[c].start()
        to_y[d].start()
    forwards = [
        pltpu.make_async_remote_copy(
            src_ref=plane.at[slot, 0], dst_ref=plane.at[slot, 1],
            send_sem=fwd_send.at[slot], recv_sem=fwd_recv.at[slot],
            device_id=partner, device_id_type=MESH,
        )
        for slot in range(PLANE)
    ]
    forwards[0].start()

    def relay_far(c):
        @pl.when(z == 2)
        def _():
            move(far.at[2], far.at[2], 5, 5, c, pair).wait_recv()
            relay_transit(c).start()

        to_pair[c].wait_recv()

        @pl.when(inner)
        def _():
            relay_pair(c).start()

    query = plane[0, 0]
    sim = against(query, query)
    key_id = lax.broadcasted_iota(jnp.int32, sim.shape, 0)
    query_id = lax.broadcasted_iota(jnp.int32, sim.shape, 1)
    sim_own[0:rows] = jnp.where(key_id == query_id, -2.0, sim)
    forwards[0].wait_recv()
    sim_own[rows:] = against(plane[0, 1], query)
    take_in(sim_own, 2 * rows, rows, own_state, True)

    for c, d in zip(order, backward):
        to_x[c].wait_recv()
        if c < CHUNKS - 1:
            relay_xy[c].start()
        to_y[d].wait_recv()
        if d == CHUNKS - 1:
            relay_xy[d].start()
        relay_far(c)
    forwards[1].start()
    forwards[2].start()

    for slot in (1, 2):
        forwards[slot].wait_recv()
        sim_own[...] = against(plane[slot].reshape(2 * rows, width), query)
        take_in(sim_own, 2 * rows, rows, own_state, False)
    for copy in relay_xy:
        copy.wait_recv()
    forwards[3].start()
    forwards[3].wait_recv()
    sim_own[...] = against(plane[3].reshape(2 * rows, width), query)
    take_in(sim_own, 2 * rows, rows, own_state, False)

    lanes = 2 * PLANE * rows

    def plane_rows():
        return plane[...].reshape(lanes, width)

    sim_pair[...] = against(far[0], plane_rows())
    take_in(sim_pair, rows, lanes, plane_state, True)

    for c in range(CHUNKS - 1):
        arrives[c].wait_recv()
    head = rows - step
    if head:
        sim_pair[0:head] = against(far[1, 0:head], plane_rows())
        take_in(sim_pair, head, lanes, plane_state, False)
    arrives[-1].wait_recv()
    sim_cross[...] = against(plane_rows(), far[1])
    take_in(sim_cross, lanes, rows, cross_state, True)

    def give(slot, device):
        gift = pltpu.make_async_remote_copy(
            src_ref=result.at[slot], dst_ref=arrived.at[slot],
            send_sem=res_send.at[slot], recv_sem=res_recv.at[slot],
            device_id=device, device_id_type=MESH,
        )
        gift.start()
        return gift

    last = 2 * PLANE
    best, count = across_rows([cross_state[k] for k in range(TOPK)], cross_state[TOPK])
    result[last, 0, :, 0:rows] = best
    result[last, 1, :, 0:rows] = count
    gifts = [give(last, source)]

    sim_last[...] = against(far[1, head:rows], plane_rows())
    take_in(sim_last, step, lanes, plane_state, False)
    for start in range(0, lanes, LANES):
        tile = slice(start, start + LANES)
        best, count = across_rows([plane_state[k, :, tile] for k in range(TOPK)], plane_state[TOPK, :, tile])
        whole[0, :, tile] = best
        whole[1, :, tile] = count
    for slot in (6, 7, 2, 3, 4, 5, 1):
        result[slot, :, :, 0:rows] = whole[:, :, slot * rows : (slot + 1) * rows]
        chip = (x, y), (1 - x, y), (x, 1 - y), (1 - x, 1 - y)
        gifts.append(give(slot, place(*chip[slot // 2], z, slot % 2)))

    best, count = across_rows([own_state[k] for k in range(TOPK)], own_state[TOPK])
    lists = [best, whole[0, :, 0:rows]]
    count = count + whole[1, :, 0:rows]
    for gift, slot in zip(gifts, (last, 6, 7, 2, 3, 4, 5, 1)):
        gift.wait_recv()
        lists.append(arrived[slot, 0, :, 0:rows])
        count = count + arrived[slot, 1, :, 0:rows]
    best = merged(in_order(lists[:TOPK]), in_order(lists[TOPK:]))
    out_ref[0, :, 0:rows], _ = across_rows(best, None)
    out_ref[1, :, 0:rows] = count

    for copy in [*to_x, *to_y, *to_pair, *relay_xy, *forwards, *gifts]:
        copy.wait_send()

    @pl.when(inner)
    def _():
        for c in order:
            to_middle(c).wait_send()
            relay_pair(c).wait_send()

    @pl.when(z == 2)
    def _():
        for c in order:
            relay_transit(c).wait_send()


def direct_body(embeddings):
    rows, width = embeddings.shape
    f32 = jnp.float32
    wide = -(-rows // LANES) * LANES
    lanes = 2 * PLANE * rows
    dma = pltpu.SemaphoreType.DMA
    out = pl.pallas_call(
        direct_kernel,
        out_shape=jax.ShapeDtypeStruct((2, SUB, wide), f32),
        in_specs=[pl.BlockSpec(memory_space=pl.ANY)],
        out_specs=pl.BlockSpec(memory_space=pltpu.VMEM),
        scratch_shapes=[
            pltpu.VMEM((rows, width), embeddings.dtype),
            pltpu.VMEM((PLANE, 2, rows, width), jnp.bfloat16),
            pltpu.VMEM((3, rows, width), jnp.bfloat16),
            pltpu.VMEM((2 * rows, rows), f32),
            pltpu.VMEM((rows, lanes), f32),
            pltpu.VMEM((lanes, rows), f32),
            pltpu.VMEM((rows // CHUNKS, lanes), f32),
            pltpu.VMEM((TOPK + 1, SUB, rows), f32),
            pltpu.VMEM((TOPK + 1, SUB, lanes), f32),
            pltpu.VMEM((TOPK + 1, SUB, rows), f32),
            pltpu.VMEM((2, SUB, lanes), f32),
            pltpu.VMEM((2 * PLANE + 1, 2, SUB, wide), f32),
            pltpu.VMEM((2 * PLANE + 1, 2, SUB, wide), f32),
            dma,
            dma((7, CHUNKS)),
            dma((6, CHUNKS)),
            dma((PLANE,)),
            dma((PLANE,)),
            dma((2 * PLANE + 1,)),
            dma((2 * PLANE + 1,)),
        ],
        compiler_params=pltpu.CompilerParams(collective_id=0, has_side_effects=True),
    )(embeddings)
    return out[0, :, :rows].T, out[1, 0, :rows]


def solution(mesh):
    placed = (P(("blk", "rep"), None),)
    direct = all(mesh.shape[axis] == size for axis, size in PLAN.items())
    return jax.shard_map(
        direct_body if direct else body,
        mesh=mesh,
        in_specs=placed,
        out_specs=(P(("blk", "rep"), None), P(("blk", "rep"))),
        check_vma=False,
    )
```

profile of v0, /device:TPU:0, one launch (start us, length us, event | category | flops | bytes accessed | tf_op | source)
XLA Modules:
  0.0 25.3 jit_solution(5149577364158449231)
XLA Ops:
  0.6 22.2 %shard_map.30 = f32[2,8,128]{2,1,0:T(8,128)} custom-call(bf16[96,1024]{1,0:T(8,128)(2,1)} %x_ref.1), custom_call_target="tpu_custom_call" | custom-call | tf_op jit(solution)/shard_map/pallas_call | solution.py:389
  22.9 1.2 %slice_bitcast_fusion.1 = f32[96]{0:T(128)} fusion(f32[2,8,128]{2,1,0:T(8,128)} %shard_map.30), kind=kLoop, calls=%fused_computation.1 | loop fusion | bytes 768 | tf_op jit(solution)/shard_map/squeeze | solution.py:418
  24.1 1.3 %slice_bitcast_fusion = f32[96,8]{0,1:T(8,128)} fusion(f32[2,8,128]{2,1,0:T(8,128)} %shard_map.30), kind=kLoop, calls=%fused_computation | loop fusion | bytes 6144 | tf_op jit(solution)/shard_map/transpose | solution.py:418
where the time goes:
time: 25.5 us; the launch traced here: 25.3 us
  Pallas kernels  22.2 us (87%)
  local copies, waits for them, and re-layouts  2.47 us (10%)
  between operations  0.64 us (3%)
    pallas_call x1, Pallas kernels, direct_body(): pl.pallas_call(direct_kernel, out_shape=jax.ShapeDtypeStruct((2, SUB, wid...  22.2 us
    transpose x1, local copies, waits for them, and re-layouts, direct_body(): return (out[0, :, :rows].T, out[1, 0, :rows])  1.27 us
    squeeze x1, local copies, waits for them, and re-layouts, direct_body(): return (out[0, :, :rows].T, out[1, 0, :rows])  1.19 us

commit v1 on v0

--- a/solution.py
+++ b/solution.py
@@ -174,7 +174,7 @@
 
 
 def direct_kernel(
-    x_ref, out_ref, raw, plane, far, sim_own, sim_pair, sim_cross, sim_last,
+    x_ref, near_ref, dup_ref, raw, plane, far, sim_own, sim_pair, sim_cross, sim_last,
     own_state, plane_state, cross_state, whole, result, arrived,
     raw_sem, send, recv, fwd_send, fwd_recv, res_send, res_recv,
 ):
@@ -362,8 +362,8 @@
         lists.append(arrived[slot, 0, :, 0:rows])
         count = count + arrived[slot, 1, :, 0:rows]
     best = merged(in_order(lists[:TOPK]), in_order(lists[TOPK:]))
-    out_ref[0, :, 0:rows], _ = across_rows(best, None)
-    out_ref[1, :, 0:rows] = count
+    near_ref[...], _ = across_rows(best, None)
+    dup_ref[...] = count[0]
 
     for copy in [*to_x, *to_y, *to_pair, *relay_xy, *forwards, *gifts]:
         copy.wait_send()
@@ -378,6 +378,17 @@
     def _():
         for c in order:
             relay_transit(c).wait_send()
+
+
+def hand_out(near_ref, dup_ref, near_out, dup_out, sems):
+    copies = [
+        pltpu.make_async_copy(src, dst, sems.at[i])
+        for i, (src, dst) in enumerate(((near_ref, near_out), (dup_ref, dup_out)))
+    ]
+    for copy in copies:
+        copy.start()
+    for copy in copies:
+        copy.wait()
 
 
 def direct_body(embeddings):
@@ -388,9 +399,9 @@
     dma = pltpu.SemaphoreType.DMA
     out = pl.pallas_call(
         direct_kernel,
-        out_shape=jax.ShapeDtypeStruct((2, SUB, wide), f32),
+        out_shape=(pltpu.VMEM((SUB, rows), f32), pltpu.VMEM((rows,), f32)),
         in_specs=[pl.BlockSpec(memory_space=pl.ANY)],
-        out_specs=pl.BlockSpec(memory_space=pltpu.VMEM),
+        out_specs=(pl.BlockSpec(memory_space=pltpu.VMEM),) * 2,
         scratch_shapes=[
             pltpu.VMEM((rows, width), embeddings.dtype),
             pltpu.VMEM((PLANE, 2, rows, width), jnp.bfloat16),
@@ -415,7 +426,14 @@
         ],
         compiler_params=pltpu.CompilerParams(collective_id=0, has_side_effects=True),
     )(embeddings)
-    return out[0, :, :rows].T, out[1, 0, :rows]
+    near, dup = pl.pallas_call(
+        hand_out,
+        out_shape=(jax.ShapeDtypeStruct((SUB, rows), f32), jax.ShapeDtypeStruct((rows,), f32)),
+        in_specs=[pl.BlockSpec(memory_space=pltpu.VMEM)] * 2,
+        out_specs=(pl.BlockSpec(memory_space=pl.ANY),) * 2,
+        scratch_shapes=[dma((2,))],
+    )(*(pltpu.with_memory_space_constraint(part, pltpu.VMEM) for part in out))
+    return near.T, dup
 
 
 def solution(mesh):

time: 25.5 us -> 23 us (0.902)
  local copies, waits for them, and re-layouts: 2.47 us -> 0 us
    transpose x1 -> x0, local copies, waits for them, and re-layouts: 1.27 us -> none  [direct_body(): return (out[0, :, :rows].T, out[1, 0, :rows])]
    squeeze x1 -> x0, local copies, waits for them, and re-layouts: 1.19 us -> none  [direct_body(): return (out[0, :, :rows].T, out[1, 0, :rows])]
    pallas_call x1 -> x2, Pallas kernels: 22.2 us -> 22.2 us  [the longest x1 21.6 us: direct_body(): pl.pallas_call(direct_kernel, out_shape=(pltpu.VMEM((SUB, rows), f32), pl...]
where the time goes in v1:
time: 23 us; the launch traced here: 22.9 us
  Pallas kernels  22.2 us (97%)
  between operations  0.64 us (3%)
    pallas_call x1, Pallas kernels, direct_body(): pl.pallas_call(direct_kernel, out_shape=(pltpu.VMEM((SUB, rows), f32), pl...  21.6 us
    pallas_call x1, Pallas kernels, direct_body(): pl.pallas_call(hand_out, out_shape=(jax.ShapeDtypeStruct((SUB, rows), f32...  0.61 us

profile of v1, /device:TPU:0, one launch (start us, length us, event | category | flops | bytes accessed | tf_op | source)
XLA Modules:
  0.0 22.9 jit_solution(6395350678958223031)
XLA Ops:
  0.6 21.6 %shard_map.30 = (f32[8,96]{1,0:T(8,128)S(1)}, f32[96]{0:T(128)S(1)}) custom-call(bf16[96,1024]{1,0:T(8,128)(2,1)} %x_ref.1), custom_call_target="tpu_custom_call" | custom-call | tf_op jit(solution)/shard_map/pallas_call | solution.py:400
  22.3 0.6 %shard_map.31 = (f32[8,96]{1,0:T(8,128)}, f32[96]{0:T(128)}) custom-call(f32[8,96]{1,0:T(8,128)S(1)} %get-tuple-element.6.near_ref, f32[96]{0:T(128)S(1)} %get-tuple-element.7.dup_ref), custom_call_target="tpu_custom_call" | custom-call | tf_op jit(solution)/shard_map/pallas_call | solution.py:429
